TPU v7x, 8 devices: a whole 2x2x1 slice. The times are simulated.
8 devices in a mesh: data: 1 (over z), model: 2 (over y), time: 4 (over x, core).
Axes of the slice: x: 2, y: 2, z: 1, core: 2. Of those that a mesh axis runs over, the one named last changes fastest.
Arguments:
- x_init: float32 [64, 256, 16], P('data')
- w_up: bfloat16 [16, 384], P(None, 'model')
- w_down: bfloat16 [384, 16], P('model')
- mod_scale: bfloat16 [32, 384], P('time', 'model')
- mod_shift: bfloat16 [32, 384], P('time', 'model')
- step_size: float32 [32], P('time')
Outputs:
- output: float32 [32, 64, 256, 16], P('time', 'data')
All inputs are finite; a program needn't handle non-finite values.
Results may differ from a plain program's by a relative error of at most 0.001.
Values are sent between devices in bfloat16 or wider.
A program may use at most 1 GiB of HBM per device.

v0:
```python
import jax
import jax.numpy as jnp
from jax import lax
from jax.sharding import PartitionSpec as P

SWEEPS = 4


def local_drift(latents, w_up, w_down, scale_f, shift_f):
    pre_act = jnp.einsum('tbnc,cd->tbnd', latents.astype(jnp.bfloat16), w_up, preferred_element_type=jnp.float32)
    hidden = jax.nn.gelu(pre_act * scale_f[:, None, None, :] + shift_f[:, None, None, :], approximate=True)
    return jnp.einsum('tbnd,dc->tbnc', hidden.astype(jnp.bfloat16), w_down, preferred_element_type=jnp.float32)


def solution(mesh):
    time_devs = mesh.shape['time']

    def device_body(x_init, w_up, w_down, mod_scale, mod_shift, step_size):
        scale_f = 1.0 + mod_scale.astype(jnp.float32)
        shift_f = mod_shift.astype(jnp.float32)
        step_col = step_size[:, None, None, None]
        latents = jnp.broadcast_to(x_init[None], (mod_scale.shape[0],) + x_init.shape)
        for sweep_idx in range(SWEEPS):
            part_drift = local_drift(latents, w_up, w_down, scale_f, shift_f)
            drifts = step_col * lax.psum(part_drift, 'model')
            running = jnp.cumsum(drifts, axis=0)
            dev_total = running[-1]
            scan_acc = dev_total
            shift_len = 1
            while shift_len < time_devs:
                perm_pairs = [(source_idx, source_idx + shift_len) for source_idx in range(time_devs - shift_len)]
                scan_acc = scan_acc + lax.ppermute(scan_acc, 'time', perm_pairs)
                shift_len = shift_len * 2
            offset = scan_acc - dev_total
            latents = (x_init + offset)[None] + (running - drifts)
        return latents

    return jax.shard_map(device_body, mesh=mesh, in_specs=(P('data', None, None), P(None, 'model'), P('model', None), P('time', 'model'), P('time', 'model'), P('time')), out_specs=P('time', 'data', None, None), check_vma=False)
```

profile of v0, /device:TPU:0, one launch (start us, length us, event | category | flops | bytes accessed | tf_op | source)
XLA Modules:
  0.0 1210.5 jit_solution(12297370469469285374)
XLA Ops:
  6.5 0.0 copy-start
  6.5 0.0 all-reduce.5.cloned.1.call-start
  6.5 0.7 convert_add_fusion
  7.2 0.7 convert_element_type.33
  7.9 1.3 convert_element_type.31
  9.2 0.0 copy-done
  9.2 46.4 %fusion.38 = f32[8,64,256,16]{2,3,1,0:T(8,128)} fusion(f32[8,192]{1,0:T(8,128)S(1)} %convert_element_type.33, f32[8,192]{1,0:T(8,128)S(1)} %convert_add_fusion, bf16[64,256,16]{1,2,0:T(8,128)(2,1)S(1)} %convert_element_type.31, bf16[192,16]{0,1:T(8,128)(2,1)S(1)} %copy-done, bf16[16,192]{1,0:T(8,128)(2,1)} %param.7), kind=kOutput, calls=%fused_computation.39 | convolution fusion | flops 1887436800 | bytes 8937472 | tf_op jit(solution)/shard_map/tbnd,dc->tbnc/dot_general | solution.py:12
  55.6 0.0 copy-start.2
  55.6 0.0 all-reduce.5.cloned.1.call-update
  55.6 0.0 copy-start.1
  55.6 0.0 all-reduce.7.cloned.1.call-start
  55.7 195.1 %all-reduce.5.cloned.1.call-done = f32[8,64,256,16]{2,3,1,0:T(8,128)} async-done(((f32[8,64,256,16]{2,3,1,0:T(8,128)}), f32[8,64,256,16]{2,3,1,0:T(8,128)}) %all-reduce.5.cloned.1.call-update) | async-done | bytes 8388624 | tf_op jit(solution)/shard_map/psum | solution.py:25
  250.8 0.0 copy-done.2
  250.8 8.2 fusion.54
  259.0 0.0 copy-start.3
  259.0 1.3 slice_bitcast_fusion.3
  260.3 1.6 collective-permute-start
  261.9 2.2 collective-permute-done
  264.1 1.5 fusion.102
  265.6 16.0 %collective-permute-start.1 = (f32[64,256,16]{1,2,0:T(8,128)S(1)}, f32[64,256,16]{1,2,0:T(8,128)S(1)}, u32[]{:S(2)}, u32[]{:S(2)}) collective-permute-start(f32[64,256,16]{1,2,0:T(8,128)S(1)} %fusion.102), channel_id=1, source_target_pairs={{0,2},{1,3},{4,6},{5,7}} | collective-permute-start | bytes 3145736 | tf_op jit(solution)/shard_map/ppermute | solution.py:32
  281.6 19.5 %collective-permute-done.1 = f32[64,256,16]{1,2,0:T(8,128)S(1)} collective-permute-done((f32[64,256,16]{1,2,0:T(8,128)S(1)}, f32[64,256,16]{1,2,0:T(8,128)S(1)}, u32[]{:S(2)}, u32[]{:S(2)}) %collective-permute-start.1) | collective-permute-done | bytes 1048608 | tf_op jit(solution)/shard_map/ppermute | solution.py:32
  301.1 0.0 copy-done.1
  301.1 1.7 subtract_add_fusion.4
  302.8 0.0 copy-done.3
  302.8 50.6 %fusion.36 = f32[8,64,256,16]{2,3,1,0:T(8,128)} fusion(f32[8,192]{1,0:T(8,128)S(1)} %convert_element_type.33, f32[8,192]{1,0:T(8,128)S(1)} %convert_add_fusion, f32[8,64,256,16]{2,3,1,0:T(8,128)} %fusion.54, f32[8,64,256,16]{2,3,1,0:T(8,128)} %all-reduce.5.cloned.1.call-done, f32[64,256,16]{1,2,0:T(8,128)S(1)} %subtract_add_fusion.4, f32[8]{0:T(128)S(1)} %copy-done.2, ...), kind=kOutput, calls=%fused_computation.38 | convolution fusion | flops 1895825408 | bytes 26239008 | tf_op jit(solution)/shard_map/tbnd,dc->tbnc/dot_general | solution.py:12
  353.4 0.0 all-reduce.7.cloned.1.call-update
  353.4 9.7 all-reduce.9.cloned.1.call-start
  363.1 184.0 %all-reduce.7.cloned.1.call-done = f32[8,64,256,16]{2,3,1,0:T(8,128)} async-done(((f32[8,64,256,16]{2,3,1,0:T(8,128)}), f32[8,64,256,16]{2,3,1,0:T(8,128)}) %all-reduce.7.cloned.1.call-update) | async-done | bytes 8388624 | tf_op jit(solution)/shard_map/psum | solution.py:25
  547.2 8.2 fusion.52
  555.4 1.3 slice_bitcast_fusion.2
  556.7 1.6 collective-permute-start.2
  558.3 2.2 collective-permute-done.2
  560.5 1.5 fusion.103
  561.9 15.8 %collective-permute-start.3 = (f32[64,256,16]{1,2,0:T(8,128)S(1)}, f32[64,256,16]{1,2,0:T(8,128)S(1)}, u32[]{:S(2)}, u32[]{:S(2)}) collective-permute-start(f32[64,256,16]{1,2,0:T(8,128)S(1)} %fusion.103), channel_id=1, source_target_pairs={{0,2},{1,3},{4,6},{5,7}} | collective-permute-start | bytes 3145736 | tf_op jit(solution)/shard_map/ppermute | solution.py:32
  577.7 19.8 %collective-permute-done.3 = f32[64,256,16]{1,2,0:T(8,128)S(1)} collective-permute-done((f32[64,256,16]{1,2,0:T(8,128)S(1)}, f32[64,256,16]{1,2,0:T(8,128)S(1)}, u32[]{:S(2)}, u32[]{:S(2)}) %collective-permute-start.3) | collective-permute-done | bytes 1048608 | tf_op jit(solution)/shard_map/ppermute | solution.py:32
  597.5 1.7 subtract_add_fusion.3
  599.2 50.6 %fusion.34 = f32[8,64,256,16]{2,3,1,0:T(8,128)} fusion(f32[8,192]{1,0:T(8,128)S(1)} %convert_element_type.33, f32[8,192]{1,0:T(8,128)S(1)} %convert_add_fusion, f32[8,64,256,16]{2,3,1,0:T(8,128)} %fusion.52, f32[8,64,256,16]{2,3,1,0:T(8,128)} %all-reduce.7.cloned.1.call-done, f32[64,256,16]{1,2,0:T(8,128)S(1)} %subtract_add_fusion.3, f32[8]{0:T(128)S(1)} %copy-done.2, ...), kind=kOutput, calls=%fused_computation.37 | convolution fusion | flops 1895825408 | bytes 26239008 | tf_op jit(solution)/shard_map/tbnd,dc->tbnc/dot_general | solution.py:12
  649.7 0.0 all-reduce.9.cloned.1.call-update
  649.8 0.3 all-reduce.11.cloned.1.call-start
  650.0 193.5 %all-reduce.9.cloned.1.call-done = f32[8,64,256,16]{2,3,1,0:T(8,128)} async-done(((f32[8,64,256,16]{2,3,1,0:T(8,128)}), f32[8,64,256,16]{2,3,1,0:T(8,128)}) %all-reduce.9.cloned.1.call-update) | async-done | bytes 8388624 | tf_op jit(solution)/shard_map/psum | solution.py:25
  843.5 8.2 fusion.50
  851.7 1.3 slice_bitcast_fusion.1
  853.0 1.6 collective-permute-start.4
  854.6 2.2 collective-permute-done.4
  856.8 1.5 fusion.104
  858.3 15.8 %collective-permute-start.5 = (f32[64,256,16]{1,2,0:T(8,128)S(1)}, f32[64,256,16]{1,2,0:T(8,128)S(1)}, u32[]{:S(2)}, u32[]{:S(2)}) collective-permute-start(f32[64,256,16]{1,2,0:T(8,128)S(1)} %fusion.104), channel_id=1, source_target_pairs={{0,2},{1,3},{4,6},{5,7}} | collective-permute-start | bytes 3145736 | tf_op jit(solution)/shard_map/ppermute | solution.py:32
  874.1 19.8 %collective-permute-done.5 = f32[64,256,16]{1,2,0:T(8,128)S(1)} collective-permute-done((f32[64,256,16]{1,2,0:T(8,128)S(1)}, f32[64,256,16]{1,2,0:T(8,128)S(1)}, u32[]{:S(2)}, u32[]{:S(2)}) %collective-permute-start.5) | collective-permute-done | bytes 1048608 | tf_op jit(solution)/shard_map/ppermute | solution.py:32
  893.8 1.7 subtract_add_fusion.2
  895.5 50.8 %fusion.32 = f32[8,64,256,16]{2,3,1,0:T(8,128)} fusion(f32[8,192]{1,0:T(8,128)S(1)} %convert_element_type.33, f32[8,192]{1,0:T(8,128)S(1)} %convert_add_fusion, f32[8,64,256,16]{2,3,1,0:T(8,128)} %fusion.50, f32[8,64,256,16]{2,3,1,0:T(8,128)} %all-reduce.9.cloned.1.call-done, f32[64,256,16]{1,2,0:T(8,128)S(1)} %subtract_add_fusion.2, f32[8]{0:T(128)S(1)} %copy-done.2, ...), kind=kOutput, calls=%fused_computation.36 | convolution fusion | flops 1895825408 | bytes 26239008 | tf_op jit(solution)/shard_map/tbnd,dc->tbnc/dot_general | solution.py:12
  946.3 0.0 all-reduce.11.cloned.1.call-update
  946.3 193.7 %all-reduce.11.cloned.1.call-done = f32[8,64,256,16]{2,3,1,0:T(8,128)} async-done(((f32[8,64,256,16]{2,3,1,0:T(8,128)}), f32[8,64,256,16]{2,3,1,0:T(8,128)}) %all-reduce.11.cloned.1.call-update) | async-done | bytes 8388624 | tf_op jit(solution)/shard_map/psum | solution.py:25
  1140.1 8.2 fusion.48
  1148.3 1.3 slice_bitcast_fusion
  1149.6 1.6 collective-permute-start.6
  1151.2 2.2 collective-permute-done.6
  1153.4 1.5 fusion.105
  1154.9 15.8 %collective-permute-start.7 = (f32[64,256,16]{1,2,0:T(8,128)S(1)}, f32[64,256,16]{1,2,0:T(8,128)S(1)}, u32[]{:S(2)}, u32[]{:S(2)}) collective-permute-start(f32[64,256,16]{1,2,0:T(8,128)S(1)} %fusion.105), channel_id=1, source_target_pairs={{0,2},{1,3},{4,6},{5,7}} | collective-permute-start | bytes 3145736 | tf_op jit(solution)/shard_map/ppermute | solution.py:32
  1170.7 19.8 %collective-permute-done.7 = f32[64,256,16]{1,2,0:T(8,128)S(1)} collective-permute-done((f32[64,256,16]{1,2,0:T(8,128)S(1)}, f32[64,256,16]{1,2,0:T(8,128)S(1)}, u32[]{:S(2)}, u32[]{:S(2)}) %collective-permute-start.7) | collective-permute-done | bytes 1048608 | tf_op jit(solution)/shard_map/ppermute | solution.py:32
  1190.4 1.7 subtract_add_fusion.1
  1192.1 11.5 subtract_add_fusion
Async XLA Ops:
  6.5 2.7 copy-start
  6.5 244.3 %all-reduce.5.cloned.1.call-start = ((), (), s32[]{:S(2)}) async-start(), calls=%async_computation | async-start | bytes 16777216 | tf_op jit(solution)/shard_map/psum | solution.py:25
  55.6 195.2 %copy-start.2 = (f32[8]{0:T(128)S(1)}, f32[8]{0:T(128)}, u32[]{:S(2)}) copy-start(f32[8]{0:T(128)} %param.11) | copy-start | bytes 100
  55.6 245.5 %copy-start.1 = (f32[64,256,16]{1,2,0:T(8,128)S(1)}, f32[64,256,16]{1,2,0:T(8,128)}, u32[]{:S(2)}) copy-start(f32[64,256,16]{1,2,0:T(8,128)} %param.6) | copy-start | bytes 3145732
  55.6 491.5 %all-reduce.7.cloned.1.call-start = ((), (), s32[]{:S(2)}) async-start(), calls=%async_computation.1 | async-start | bytes 16777216 | tf_op jit(solution)/shard_map/psum | solution.py:25
  259.0 43.8 %copy-start.3 = (bf16[16,192]{1,0:T(8,128)(2,1)S(1)}, bf16[16,192]{1,0:T(8,128)(2,1)}, u32[]{:S(2)}) copy-start(bf16[16,192]{1,0:T(8,128)(2,1)} %param.7) | copy-start | bytes 18436
  260.3 3.8 collective-permute-start
  265.6 35.5 %collective-permute-start.1 = (f32[64,256,16]{1,2,0:T(8,128)S(1)}, f32[64,256,16]{1,2,0:T(8,128)S(1)}, u32[]{:S(2)}, u32[]{:S(2)}) collective-permute-start(f32[64,256,16]{1,2,0:T(8,128)S(1)} %fusion.102), channel_id=1, source_target_pairs={{0,2},{1,3},{4,6},{5,7}} | collective-permute-start | bytes 3145736 | tf_op jit(solution)/shard_map/ppermute | solution.py:32
  353.4 490.1 %all-reduce.9.cloned.1.call-start = ((), (), s32[]{:S(2)}) async-start(), calls=%async_computation.2 | async-start | bytes 16777216 | tf_op jit(solution)/shard_map/psum | solution.py:25
  556.7 3.8 collective-permute-start.2
  561.9 35.5 %collective-permute-start.3 = (f32[64,256,16]{1,2,0:T(8,128)S(1)}, f32[64,256,16]{1,2,0:T(8,128)S(1)}, u32[]{:S(2)}, u32[]{:S(2)}) collective-permute-start(f32[64,256,16]{1,2,0:T(8,128)S(1)} %fusion.103), channel_id=1, source_target_pairs={{0,2},{1,3},{4,6},{5,7}} | collective-permute-start | bytes 3145736 | tf_op jit(solution)/shard_map/ppermute | solution.py:32
  649.8 490.3 %all-reduce.11.cloned.1.call-start = ((), (), s32[]{:S(2)}) async-start(), calls=%async_computation.3 | async-start | bytes 16777216 | tf_op jit(solution)/shard_map/psum | solution.py:25
  853.0 3.8 collective-permute-start.4
  858.3 35.5 %collective-permute-start.5 = (f32[64,256,16]{1,2,0:T(8,128)S(1)}, f32[64,256,16]{1,2,0:T(8,128)S(1)}, u32[]{:S(2)}, u32[]{:S(2)}) collective-permute-start(f32[64,256,16]{1,2,0:T(8,128)S(1)} %fusion.104), channel_id=1, source_target_pairs={{0,2},{1,3},{4,6},{5,7}} | collective-permute-start | bytes 3145736 | tf_op jit(solution)/shard_map/ppermute | solution.py:32
  1149.6 3.8 collective-permute-start.6
  1154.9 35.5 %collective-permute-start.7 = (f32[64,256,16]{1,2,0:T(8,128)S(1)}, f32[64,256,16]{1,2,0:T(8,128)S(1)}, u32[]{:S(2)}, u32[]{:S(2)}) collective-permute-start(f32[64,256,16]{1,2,0:T(8,128)S(1)} %fusion.105), channel_id=1, source_target_pairs={{0,2},{1,3},{4,6},{5,7}} | collective-permute-start | bytes 3145736 | tf_op jit(solution)/shard_map/ppermute | solution.py:32
Sparse Core Ops, SparseCore 0:
  55.7 194.9 all-reduce.4
  353.5 193.5 all-reduce.6
  649.9 193.5 all-reduce.8
  946.5 193.5 all-reduce.10
where the time goes:
time: 1220 us; the launch traced here: 1210 us
  waiting for transfers between devices  854 us (70%)
  matrix products  198 us (16%)
  starting transfers between devices  79.6 us (7%)
  other arithmetic  59.7 us (5%)
  between operations  13.7 us (1%)
    psum x4, waiting for transfers between devices, device_body(): drifts = step_col * lax.psum(part_drift, 'model')  766 us
    dot_general x4, matrix products, local_drift(): jnp.einsum('tbnd,dc->tbnc', hidden.astype(jnp.bfloat16), w_down, preferre...  198 us
    ppermute x8, waiting for transfers between devices, device_body(): scan_acc = scan_acc + lax.ppermute(scan_acc, 'time', perm_pairs)  87.6 us
    ppermute x8, starting transfers between devices, device_body(): scan_acc = scan_acc + lax.ppermute(scan_acc, 'time', perm_pairs)  69.6 us
    another operation x4, other arithmetic, device_body(): running = jnp.cumsum(drifts, axis=0)  33 us
  transfers between devices with their start and end apart: 12, of which 12 were waited for; matrix products, arithmetic and copies ran while one was open for 0% of the time, Pallas kernels for 0%

commit v1 on v0

v1 whole, which is shorter than its diff:
```python
import functools
import math

import jax
import jax.numpy as jnp
from jax import lax
from jax.experimental import pallas as pl
from jax.experimental.pallas import tpu as pltpu
from jax.sharding import PartitionSpec as P

MESH = pl.DeviceIdType.MESH
F32 = jnp.float32
BF16 = jnp.bfloat16

STEPS = 32
STEPS_DEV = 8
HALF = 192
HIDDEN = 384
CHAN = 16
TOKENS = 256
TILES = 8
GROUP = 8
GROUPS = 15
DEPTH = 128

ROOT = math.sqrt(2.0 / math.pi)
C1 = 2.0 * ROOT
C3 = 8.0 * 0.044715 * ROOT


def item(group, k):
    n = group * GROUP + k
    sweep0 = n < 31
    j = jnp.where(sweep0, n, jnp.where(n < 61, n - 30, jnp.where(n < 91, n - 60, n - 89)))
    return sweep0, j


def kernel(x_ref, w1_ref, w2_ref, g_ref, b_ref, h_ref, out_ref,
           gam, bet, w1s, w2s, hs, w1f, gamf, betf, mat, w2t, rhs, pre_a, pre_b, act_a, act_b, lat,
           psend, precv, send_sem, recv_sem):
    m = lax.axis_index("model")
    t = lax.axis_index("time")
    me = m * 4 + t

    offsets = [(dm, dt) for dm in range(2) for dt in range(4) if (dm, dt) != (0, 0)]
    peers = [(lax.rem(m + dm, 2), lax.rem(t + dt, 4)) for dm, dt in offsets]

    barrier = pltpu.get_barrier_semaphore()
    for pm, pt in peers:
        pl.semaphore_signal(barrier, inc=1, device_id={"model": pm, "time": pt}, device_id_type=MESH)
    pl.semaphore_wait(barrier, len(peers))

    copies = []

    def push(src, dst, peer):
        idx = len(copies)
        copy = pltpu.make_async_remote_copy(
            src_ref=src, dst_ref=dst, send_sem=psend.at[idx], recv_sem=precv.at[idx],
            device_id={"model": peer[0], "time": peer[1]}, device_id_type=MESH)
        copy.start()
        copies.append(copy)

    for (dm, dt), peer in zip(offsets, peers):
        push(g_ref, gam.at[m, t], peer)
        push(b_ref, bet.at[m, t], peer)
        if dt == 0:
            push(w1_ref, w1s.at[m], peer)
            push(w2_ref, w2s.at[m], peer)
        if dm == 0:
            push(h_ref, hs.at[t], peer)

    gam[m, t] = g_ref[...]
    bet[m, t] = b_ref[...]
    w1s[m] = w1_ref[...]
    w2s[m] = w2_ref[...]
    hs[t] = h_ref[...]
    w1f[...] = jnp.zeros_like(w1f)
    gamf[...] = jnp.zeros_like(gamf)
    betf[...] = jnp.zeros_like(betf)

    ones_zeros = jnp.concatenate([jnp.ones((16, TOKENS), BF16), jnp.zeros((DEPTH - 64, TOKENS), BF16)], axis=0)

    def init_slot(i, c):
        rhs[i, 48:DEPTH, :] = ones_zeros
        return c

    lax.fori_loop(0, STEPS + TILES, init_slot, 0)

    def init_tile(i, c):
        x0 = x_ref[me * TILES + i]
        lat[i, 0] = x0
        xb = x0.astype(BF16)
        for r in range(3):
            rhs[STEPS + i, 16 * r:16 * r + 16, :] = xb
        return c

    lax.fori_loop(0, TILES, init_tile, 0)

    for copy in copies:
        copy.wait()

    for mm in range(2):
        w1f[mm, :, 0:HALF] = w1s[mm].astype(F32) * 0.5
        w2t[mm] = w2s[mm].astype(F32)
        for tt in range(4):
            gamf[mm, 8 * tt:8 * tt + 8, 0:HALF] = gam[mm, tt].astype(F32)
            betf[mm, 8 * tt:8 * tt + 8, 0:HALF] = bet[mm, tt].astype(F32)

    row0 = lax.broadcasted_iota(jnp.int32, (8, 256), 0) == 0

    def prep(j, c):
        for mm in range(2):
            w = w1f[mm] * (1.0 + gamf[mm, pl.ds(j, 1), :])
            hi = w.astype(BF16).astype(F32)
            rest = w - hi
            mid = rest.astype(BF16).astype(F32)
            low = rest - mid
            shift = jnp.where(row0, 0.5 * betf[mm, pl.ds(j, 1), :], 0.0)
            cols = jnp.concatenate([hi, mid, low, shift, jnp.zeros((DEPTH - 56, 256), F32)], axis=0)
            mat[j, HALF * mm:HALF * mm + HALF, :] = cols.T[0:HALF, :].astype(BF16)
        return c

    lax.fori_loop(0, STEPS, prep, 0)

    def product1(tile, group, half, pre, i):
        sweep0, j = item(group, half * 4 + i)
        slot = jnp.where(sweep0, STEPS + tile, j)
        pre[i] = jnp.dot(mat[j], rhs[slot], preferred_element_type=F32)

    def gelu(pre, act, i):
        for r in range(0, HIDDEN, 16):
            z = pre[i, r:r + 16, :]
            u = z * (z * z * C3 + C1)
            act[i, r:r + 16, :] = z * (1.0 + jnp.tanh(u))

    def product2(act, i):
        return (jnp.dot(w2t[0], act[i, 0:HALF, :], preferred_element_type=F32)
                + jnp.dot(w2t[1], act[i, HALF:HIDDEN, :], preferred_element_type=F32))

    def update(tile, group, half, drifts):
        for i in range(4):
            _, j = item(group, half * 4 + i)
            hrow = hs[j // 8, pl.ds(lax.rem(j, 8), 1), :]
            x = lat[tile, j] + hrow * drifts[i]
            lat[tile, j + 1] = x
            xb = x.astype(BF16)
            for r in range(3):
                rhs[j + 1, 16 * r:16 * r + 16, :] = xb

    def phase_q(tile, group, next_tile, next_group, first):
        drifts = []
        for i in range(4):
            product1(next_tile, next_group, 1, pre_b, i)
            if not first:
                drifts.append(product2(act_b, i))
            gelu(pre_a, act_a, i)
        if not first:
            update(tile, group, 1, drifts)

    def phase_p(tile, group, next_tile, next_group):
        drifts = []
        for i in range(4):
            product1(next_tile, next_group, 0, pre_a, i)
            drifts.append(product2(act_a, i))
            gelu(pre_b, act_b, i)
        update(tile, group, 0, drifts)

    for i in range(4):
        product1(0, 0, 0, pre_a, i)
    phase_q(0, 0, 0, 0, True)

    def outgoing(tile, q, pm, slot):
        return pltpu.make_async_remote_copy(
            src_ref=lat.at[tile, pl.ds(q * STEPS_DEV, STEPS_DEV)],
            dst_ref=out_ref.at[:, me * TILES + tile],
            send_sem=send_sem.at[tile, q, slot],
            recv_sem=recv_sem.at[me, tile],
            device_id={"model": pm, "time": q}, device_id_type=MESH)

    def trip(tile, group, c):
        wrap = group == GROUPS - 1
        next_tile = jnp.where(wrap, jnp.minimum(tile + 1, TILES - 1), tile)
        next_group = jnp.where(wrap, 0, group + 1)
        phase_p(tile, group, next_tile, next_group)
        phase_q(tile, group, next_tile, next_group, False)

        @pl.when(group >= GROUPS - 4)
        def _():
            q = group - (GROUPS - 4)
            outgoing(tile, q, 1 - m, 0).start()

            @pl.when(q != t)
            def _():
                outgoing(tile, q, m, 1).start()

            @pl.when(q == t)
            def _():
                for r in range(STEPS_DEV):
                    out_ref[r, me * TILES + tile] = lat[tile, q * STEPS_DEV + r]

        return c

    def tile_loop(tile, c):
        return lax.fori_loop(0, GROUPS, lambda group, cc: trip(tile, group, cc), c)

    lax.fori_loop(0, TILES, tile_loop, 0)

    def finish(i, c):
        for q in range(4):
            outgoing(i, q, 1 - m, 0).wait_send()

            @pl.when(q != t)
            def _():
                outgoing(i, q, m, 1).wait_send()

        for src in range(8):
            @pl.when(src != me)
            def _():
                pltpu.make_async_remote_copy(
                    src_ref=lat.at[0, pl.ds(0, STEPS_DEV)],
                    dst_ref=out_ref.at[:, src * TILES + i],
                    send_sem=send_sem.at[0, 0, 0],
                    recv_sem=recv_sem.at[src, i],
                    device_id={"model": m, "time": t}, device_id_type=MESH).wait_recv()
        return c

    lax.fori_loop(0, TILES, finish, 0)


def solution(mesh):
    def device_body(x_init, w_up, w_down, mod_scale, mod_shift, step_size):
        batch = x_init.shape[0]
        vmem = pl.BlockSpec(memory_space=pltpu.VMEM)
        out = pl.pallas_call(
            kernel,
            out_shape=jax.ShapeDtypeStruct((STEPS_DEV, batch, CHAN, TOKENS), F32),
            in_specs=[vmem] * 6,
            out_specs=vmem,
            scratch_shapes=[
                pltpu.VMEM((2, 4, STEPS_DEV, HALF), BF16),
                pltpu.VMEM((2, 4, STEPS_DEV, HALF), BF16),
                pltpu.VMEM((2, CHAN, HALF), BF16),
                pltpu.VMEM((2, CHAN, HALF), BF16),
                pltpu.VMEM((4, STEPS_DEV, TOKENS), F32),
                pltpu.VMEM((2, CHAN, 256), F32),
                pltpu.VMEM((2, STEPS, 256), F32),
                pltpu.VMEM((2, STEPS, 256), F32),
                pltpu.VMEM((STEPS, HIDDEN, DEPTH), BF16),
                pltpu.VMEM((2, CHAN, HALF), F32),
                pltpu.VMEM((STEPS + TILES, DEPTH, TOKENS), BF16),
                pltpu.VMEM((4, HIDDEN, TOKENS), F32),
                pltpu.VMEM((4, HIDDEN, TOKENS), F32),
                pltpu.VMEM((4, HIDDEN, TOKENS), F32),
                pltpu.VMEM((4, HIDDEN, TOKENS), F32),
                pltpu.VMEM((TILES, STEPS, CHAN, TOKENS), F32),
                pltpu.SemaphoreType.DMA((19,)),
                pltpu.SemaphoreType.DMA((19,)),
                pltpu.SemaphoreType.DMA((TILES, 4, 2)),
                pltpu.SemaphoreType.DMA((8, TILES)),
            ],
            compiler_params=pltpu.CompilerParams(
                collective_id=0, has_side_effects=True, vmem_limit_bytes=60 * 1024 * 1024),
        )(x_init.transpose(0, 2, 1), w_up, w_down.T, mod_scale, mod_shift,
          jnp.broadcast_to(step_size[:, None], (STEPS_DEV, TOKENS)))
        return out.transpose(0, 1, 3, 2)

    return jax.shard_map(
        device_body, mesh=mesh,
        in_specs=(P('data', None, None), P(None, 'model'), P('model', None), P('time', 'model'), P('time', 'model'), P('time')),
        out_specs=P('time', 'data', None, None), check_vma=False)
```

time: 1220 us -> 173 us (0.14)
  waiting for transfers between devices: 854 us -> 0 us
  matrix products: 198 us -> 0 us
  Pallas kernels: 0 us -> 164 us
  starting transfers between devices: 79.6 us -> 0 us
  other arithmetic: 59.7 us -> 0 us
  between operations: 13.7 us -> 0.01 us
    psum x4 -> x0, waiting for transfers between devices: 766 us -> none  [device_body(): drifts = step_col * lax.psum(part_drift, 'model')]
    dot_general x4 -> x0, matrix products: 198 us -> none  [local_drift(): jnp.einsum('tbnd,dc->tbnc', hidden.astype(jnp.bfloat16), w_down, preferre...]
    pallas_call x0 -> x1, Pallas kernels: none -> 164 us  [device_body(): pl.pallas_call(kernel, out_shape=jax.ShapeDtypeStruct((STEPS_DEV, batch,...]
    ppermute x8 -> x0, waiting for transfers between devices: 87.6 us -> none  [device_body(): scan_acc = scan_acc + lax.ppermute(scan_acc, 'time', perm_pairs)]
    ppermute x8 -> x0, starting transfers between devices: 69.6 us -> none  [device_body(): scan_acc = scan_acc + lax.ppermute(scan_acc, 'time', perm_pairs)]
    another operation x4 -> x0, other arithmetic: 33 us -> none  [device_body(): running = jnp.cumsum(drifts, axis=0)]
    add x10 -> x0, other arithmetic: 24.8 us -> none  [the longest x5 18.1 us: device_body(): latents = (x_init + offset)[None] + (running - drifts)]
  transfers between devices with their start and end apart: 12 -> 0, of which waited for: 12 -> 0; matrix products, arithmetic and copies ran while one was open for 0% -> 0% of each run, Pallas kernels for 0% -> 0%
where the time goes in v1:
time: 173 us
  Pallas kernels  164 us (95%)
  local copies, waits for them, and re-layouts  9.08 us (5%)
    pallas_call x1, Pallas kernels, device_body(): pl.pallas_call(kernel, out_shape=jax.ShapeDtypeStruct((STEPS_DEV, batch,...  164 us
    unnamed x1, local copies, waits for them, and re-layouts  7.76 us

profile of v1, /device:TPU:0, one launch (start us, length us, event | category | flops | bytes accessed | tf_op | source)
XLA Modules:
  0.0 173.2 jit_solution(16772133741152330337)
XLA Ops:
  0.0 1.3 broadcast_in_dim.2.h_ref
  1.3 164.1 %shard_map.64 = f32[8,64,16,256]{3,2,1,0:T(8,128)} custom-call(f32[64,16,256]{2,1,0:T(8,128)} %bitcast.4, bf16[16,192]{1,0:T(8,128)(2,1)} %w1_ref.1, bf16[16,192]{1,0:T(8,128)(2,1)} %bitcast.5, bf16[8,192]{1,0:T(8,128)(2,1)} %g_ref.1, bf16[8,192]{1,0:T(8,128)(2,1)} %b_ref.1, f32[8,256]{1,0:T(8,128)} %broadcast_in_dim.2.h_ref), custom_call_target="tpu_custom_call" | custom-call | tf_op jit(solution)/shard_map/pallas_call | solution.py:234
  165.5 7.8 %copy.8 = f32[8,64,256,16]{2,3,1,0:T(8,128)} copy(f32[8,64,256,16]{2,3,1,0:T(8,128)} %bitcast.3) | data formatting | bytes 16777216

commit v2 on v1

--- a/solution.py
+++ b/solution.py
@@ -21,6 +21,7 @@
 TILES = 8
 GROUP = 8
 GROUPS = 15
+HALF_GROUP = GROUP // 2
 DEPTH = 128
 
 ROOT = math.sqrt(2.0 / math.pi)
@@ -36,7 +37,7 @@
 
 
 def kernel(x_ref, w1_ref, w2_ref, g_ref, b_ref, h_ref, out_ref,
-           gam, bet, w1s, w2s, hs, w1f, gamf, betf, mat, w2t, rhs, pre_a, pre_b, act_a, act_b, lat,
+           gam, bet, w1s, w2s, hs, hb, w1f, gamf, betf, mat, rhs, pre_a, pre_b, act_a, act_b, lat,
            psend, precv, send_sem, recv_sem):
     m = lax.axis_index("model")
     t = lax.axis_index("time")
@@ -101,10 +102,13 @@
 
     for mm in range(2):
         w1f[mm, :, 0:HALF] = w1s[mm].astype(F32) * 0.5
-        w2t[mm] = w2s[mm].astype(F32)
         for tt in range(4):
             gamf[mm, 8 * tt:8 * tt + 8, 0:HALF] = gam[mm, tt].astype(F32)
             betf[mm, 8 * tt:8 * tt + 8, 0:HALF] = bet[mm, tt].astype(F32)
+
+    for tt in range(4):
+        for r in range(STEPS_DEV):
+            hb[tt * STEPS_DEV + r] = jnp.broadcast_to(hs[tt, :, r:r + 1], (CHAN, TOKENS))
 
     row0 = lax.broadcasted_iota(jnp.int32, (8, 256), 0) == 0
 
@@ -123,7 +127,7 @@
     lax.fori_loop(0, STEPS, prep, 0)
 
     def product1(tile, group, half, pre, i):
-        sweep0, j = item(group, half * 4 + i)
+        sweep0, j = item(group, half * HALF_GROUP + i)
         slot = jnp.where(sweep0, STEPS + tile, j)
         pre[i] = jnp.dot(mat[j], rhs[slot], preferred_element_type=F32)
 
@@ -131,43 +135,40 @@
         for r in range(0, HIDDEN, 16):
             z = pre[i, r:r + 16, :]
             u = z * (z * z * C3 + C1)
-            act[i, r:r + 16, :] = z * (1.0 + jnp.tanh(u))
+            act[i, r:r + 16, :] = (z * (1.0 + jnp.tanh(u))).astype(BF16)
 
     def product2(act, i):
-        return (jnp.dot(w2t[0], act[i, 0:HALF, :], preferred_element_type=F32)
-                + jnp.dot(w2t[1], act[i, HALF:HIDDEN, :], preferred_element_type=F32))
-
-    def update(tile, group, half, drifts):
-        for i in range(4):
-            _, j = item(group, half * 4 + i)
-            hrow = hs[j // 8, pl.ds(lax.rem(j, 8), 1), :]
-            x = lat[tile, j] + hrow * drifts[i]
+        return (jnp.dot(w2s[0], act[i, 0:HALF, :], preferred_element_type=F32)
+                + jnp.dot(w2s[1], act[i, HALF:HIDDEN, :], preferred_element_type=F32))
+
+    def update(tile, group, drifts):
+        for i in range(GROUP):
+            _, j = item(group, i)
+            x = lat[tile, j] + hb[j] * drifts[i]
             lat[tile, j + 1] = x
             xb = x.astype(BF16)
             for r in range(3):
                 rhs[j + 1, 16 * r:16 * r + 16, :] = xb
 
-    def phase_q(tile, group, next_tile, next_group, first):
-        drifts = []
-        for i in range(4):
+    def phase_q(next_tile, next_group, first):
+        for i in range(HALF_GROUP):
             product1(next_tile, next_group, 1, pre_b, i)
-            if not first:
-                drifts.append(product2(act_b, i))
+        drifts = [] if first else [product2(act_b, i) for i in range(HALF_GROUP)]
+        for i in range(HALF_GROUP):
             gelu(pre_a, act_a, i)
-        if not first:
-            update(tile, group, 1, drifts)
-
-    def phase_p(tile, group, next_tile, next_group):
-        drifts = []
-        for i in range(4):
+        return drifts
+
+    def phase_p(next_tile, next_group):
+        for i in range(HALF_GROUP):
             product1(next_tile, next_group, 0, pre_a, i)
-            drifts.append(product2(act_a, i))
+        drifts = [product2(act_a, i) for i in range(HALF_GROUP)]
+        for i in range(HALF_GROUP):
             gelu(pre_b, act_b, i)
-        update(tile, group, 0, drifts)
-
-    for i in range(4):
+        return drifts
+
+    for i in range(HALF_GROUP):
         product1(0, 0, 0, pre_a, i)
-    phase_q(0, 0, 0, 0, True)
+    phase_q(0, 0, True)
 
     def outgoing(tile, q, pm, slot):
         return pltpu.make_async_remote_copy(
@@ -181,8 +182,9 @@
         wrap = group == GROUPS - 1
         next_tile = jnp.where(wrap, jnp.minimum(tile + 1, TILES - 1), tile)
         next_group = jnp.where(wrap, 0, group + 1)
-        phase_p(tile, group, next_tile, next_group)
-        phase_q(tile, group, next_tile, next_group, False)
+        drifts = phase_p(next_tile, next_group)
+        drifts = drifts + phase_q(next_tile, next_group, False)
+        update(tile, group, drifts)
 
         @pl.when(group >= GROUPS - 4)
         def _():
@@ -233,7 +235,7 @@
         vmem = pl.BlockSpec(memory_space=pltpu.VMEM)
         out = pl.pallas_call(
             kernel,
-            out_shape=jax.ShapeDtypeStruct((STEPS_DEV, batch, CHAN, TOKENS), F32),
+            out_shape=pltpu.VMEM((STEPS_DEV, batch, CHAN, TOKENS), F32),
             in_specs=[vmem] * 6,
             out_specs=vmem,
             scratch_shapes=[
@@ -241,17 +243,17 @@
                 pltpu.VMEM((2, 4, STEPS_DEV, HALF), BF16),
                 pltpu.VMEM((2, CHAN, HALF), BF16),
                 pltpu.VMEM((2, CHAN, HALF), BF16),
-                pltpu.VMEM((4, STEPS_DEV, TOKENS), F32),
+                pltpu.VMEM((4, 1, STEPS_DEV), F32),
+                pltpu.VMEM((STEPS, CHAN, TOKENS), F32),
                 pltpu.VMEM((2, CHAN, 256), F32),
                 pltpu.VMEM((2, STEPS, 256), F32),
                 pltpu.VMEM((2, STEPS, 256), F32),
                 pltpu.VMEM((STEPS, HIDDEN, DEPTH), BF16),
-                pltpu.VMEM((2, CHAN, HALF), F32),
                 pltpu.VMEM((STEPS + TILES, DEPTH, TOKENS), BF16),
-                pltpu.VMEM((4, HIDDEN, TOKENS), F32),
-                pltpu.VMEM((4, HIDDEN, TOKENS), F32),
-                pltpu.VMEM((4, HIDDEN, TOKENS), F32),
-                pltpu.VMEM((4, HIDDEN, TOKENS), F32),
+                pltpu.VMEM((HALF_GROUP, HIDDEN, TOKENS), F32),
+                pltpu.VMEM((HALF_GROUP, HIDDEN, TOKENS), F32),
+                pltpu.VMEM((HALF_GROUP, HIDDEN, TOKENS), BF16),
+                pltpu.VMEM((HALF_GROUP, HIDDEN, TOKENS), BF16),
                 pltpu.VMEM((TILES, STEPS, CHAN, TOKENS), F32),
                 pltpu.SemaphoreType.DMA((19,)),
                 pltpu.SemaphoreType.DMA((19,)),
@@ -259,9 +261,9 @@
                 pltpu.SemaphoreType.DMA((8, TILES)),
             ],
             compiler_params=pltpu.CompilerParams(
-                collective_id=0, has_side_effects=True, vmem_limit_bytes=60 * 1024 * 1024),
+                collective_id=0, has_side_effects=True, vmem_limit_bytes=24 * 1024 * 1024),
         )(x_init.transpose(0, 2, 1), w_up, w_down.T, mod_scale, mod_shift,
-          jnp.broadcast_to(step_size[:, None], (STEPS_DEV, TOKENS)))
+          step_size[None, :])
         return out.transpose(0, 1, 3, 2)
 
     return jax.shard_map(

time: 173 us -> 166 us (0.960)
  Pallas kernels: 164 us -> 158 us
    pallas_call x1, Pallas kernels: 164 us -> 158 us  [device_body(): pl.pallas_call(kernel, out_shape=pltpu.VMEM((STEPS_DEV, batch, CHAN, TOKE...]
    unnamed x1 -> x13, local copies, waits for them, and re-layouts: 7.76 us -> 8.04 us
where the time goes in v2:
time: 166 us
  Pallas kernels  158 us (95%)
  local copies, waits for them, and re-layouts  8.04 us (5%)
    pallas_call x1, Pallas kernels, device_body(): pl.pallas_call(kernel, out_shape=pltpu.VMEM((STEPS_DEV, batch, CHAN, TOKE...  158 us
    unnamed x13, local copies, waits for them, and re-layouts  8.04 us

profile of v2, /device:TPU:0, one launch (start us, length us, event | category | flops | bytes accessed | tf_op | source)
XLA Modules:
  0.0 165.9 jit_solution(7703240867356194955)
XLA Ops:
  0.0 0.0 copy-start
  0.0 1.2 copy-done
  1.2 0.0 copy-start.1
  1.2 0.7 copy-done.1
  1.9 0.0 copy-start.2
  1.9 0.7 copy-done.2
  2.6 0.0 copy-start.3
  2.6 0.7 copy-done.3
  3.3 0.0 copy-start.4
  3.3 0.7 copy-done.4
  4.0 0.0 copy-start.5
  4.0 0.7 copy-done.5
  4.7 157.8 %shard_map.64 = f32[8,64,16,256]{3,2,1,0:T(8,128)S(1)} custom-call(f32[64,16,256]{2,1,0:T(8,128)S(1)} %bitcast.5, bf16[16,192]{1,0:T(8,128)(2,1)S(1)} %copy-done.1, bf16[16,192]{1,0:T(8,128)(2,1)S(1)} %bitcast.6, bf16[8,192]{1,0:T(8,128)(2,1)S(1)} %copy-done.3, bf16[8,192]{1,0:T(8,128)(2,1)S(1)} %copy-done.4, f32[1,8]{1,0:T(1,128)S(1)} %bitcast.7), custom_call_target="tpu_custom_call" | custom-call | tf_op jit(solution)/shard_map/pallas_call | solution.py:236
  162.5 3.4 %copy.8 = f32[8,64,256,16]{2,3,1,0:T(8,128)} copy(f32[8,64,256,16]{2,3,1,0:T(8,128)S(1)} %bitcast.4) | data formatting | bytes 16777216
Async XLA Ops:
  0.0 1.2 copy-start
  1.2 0.7 copy-start.1
  1.9 0.7 copy-start.2
  2.6 0.7 copy-start.3
  3.3 0.7 copy-start.4
  4.0 0.7 copy-start.5

commit v3 on v2

--- a/solution.py
+++ b/solution.py
@@ -21,8 +21,8 @@
 TILES = 8
 GROUP = 8
 GROUPS = 15
-HALF_GROUP = GROUP // 2
 DEPTH = 128
+ORDER = ('g0 p0 p1 g1 ' 'q0 q1 p2 g2 ' 'p3 q2 q3 g3 ' 'p4 p5 g4 p6 ' 'g5 p7 g6 g7')
 
 ROOT = math.sqrt(2.0 / math.pi)
 C1 = 2.0 * ROOT
@@ -37,14 +37,20 @@
 
 
 def kernel(x_ref, w1_ref, w2_ref, g_ref, b_ref, h_ref, out_ref,
-           gam, bet, w1s, w2s, hs, hb, w1f, gamf, betf, mat, rhs, pre_a, pre_b, act_a, act_b, lat,
-           psend, precv, send_sem, recv_sem):
+           gam, bet, w1s, w2s, hs, hb, w1f, gamf, betf, mat, rhs, w2p, xs, pre_a, pre_b, act_a, act_b, lat,
+           own_sem, psend, precv, send_sem, recv_sem):
     m = lax.axis_index("model")
     t = lax.axis_index("time")
     me = m * 4 + t
 
     offsets = [(dm, dt) for dm in range(2) for dt in range(4) if (dm, dt) != (0, 0)]
     peers = [(lax.rem(m + dm, 2), lax.rem(t + dt, 4)) for dm, dt in offsets]
+
+    local = [pltpu.make_async_copy(src, dst, own_sem.at[i]) for i, (src, dst) in enumerate([
+        (g_ref, gam.at[m, t]), (b_ref, bet.at[m, t]), (w1_ref, w1s.at[m]), (w2_ref, w2s.at[m]), (h_ref, hs.at[t]),
+        (x_ref.at[pl.ds(me * TILES, TILES)], xs)])]
+    for copy in local:
+        copy.start()
 
     barrier = pltpu.get_barrier_semaphore()
     for pm, pt in peers:
@@ -70,12 +76,8 @@
         if dm == 0:
             push(h_ref, hs.at[t], peer)
 
-    gam[m, t] = g_ref[...]
-    bet[m, t] = b_ref[...]
-    w1s[m] = w1_ref[...]
-    w2s[m] = w2_ref[...]
-    hs[t] = h_ref[...]
     w1f[...] = jnp.zeros_like(w1f)
+    w2p[...] = jnp.zeros_like(w2p)
     gamf[...] = jnp.zeros_like(gamf)
     betf[...] = jnp.zeros_like(betf)
 
@@ -87,8 +89,11 @@
 
     lax.fori_loop(0, STEPS + TILES, init_slot, 0)
 
+    for copy in local:
+        copy.wait()
+
     def init_tile(i, c):
-        x0 = x_ref[me * TILES + i]
+        x0 = xs[i]
         lat[i, 0] = x0
         xb = x0.astype(BF16)
         for r in range(3):
@@ -102,6 +107,8 @@
 
     for mm in range(2):
         w1f[mm, :, 0:HALF] = w1s[mm].astype(F32) * 0.5
+        for u in range(2):
+            w2p[CHAN * u:CHAN * u + CHAN, 256 * u + 128 * mm:256 * u + 128 * mm + 128] = w2s[mm][:, 0:128]
         for tt in range(4):
             gamf[mm, 8 * tt:8 * tt + 8, 0:HALF] = gam[mm, tt].astype(F32)
             betf[mm, 8 * tt:8 * tt + 8, 0:HALF] = bet[mm, tt].astype(F32)
@@ -109,6 +116,10 @@
     for tt in range(4):
         for r in range(STEPS_DEV):
             hb[tt * STEPS_DEV + r] = jnp.broadcast_to(hs[tt, :, r:r + 1], (CHAN, TOKENS))
+
+    tails = jnp.concatenate([w2s[mm].astype(F32)[:, 128:HALF] for mm in range(2)], axis=1).astype(BF16)
+    for u in range(2):
+        w2p[CHAN * u:CHAN * u + CHAN, 512 + 128 * u:640 + 128 * u] = tails
 
     row0 = lax.broadcasted_iota(jnp.int32, (8, 256), 0) == 0
 
@@ -126,20 +137,23 @@
 
     lax.fori_loop(0, STEPS, prep, 0)
 
-    def product1(tile, group, half, pre, i):
-        sweep0, j = item(group, half * HALF_GROUP + i)
+    def product1(tile, group, pre, i):
+        sweep0, j = item(group, i)
         slot = jnp.where(sweep0, STEPS + tile, j)
         pre[i] = jnp.dot(mat[j], rhs[slot], preferred_element_type=F32)
 
     def gelu(pre, act, i):
+        u = i % 2
         for r in range(0, HIDDEN, 16):
+            part, k = r // HALF, r % HALF
+            row = u * 256 + part * 128 + k if k < 128 else 512 + u * 128 + part * 64 + k - 128
             z = pre[i, r:r + 16, :]
-            u = z * (z * z * C3 + C1)
-            act[i, r:r + 16, :] = (z * (1.0 + jnp.tanh(u))).astype(BF16)
-
-    def product2(act, i):
-        return (jnp.dot(w2s[0], act[i, 0:HALF, :], preferred_element_type=F32)
-                + jnp.dot(w2s[1], act[i, HALF:HIDDEN, :], preferred_element_type=F32))
+            f = z * (z * z * C3 + C1)
+            act[i // 2, row:row + 16, :] = (z * (1.0 + jnp.tanh(f))).astype(BF16)
+
+    def product2(act, pair):
+        both = jnp.dot(w2p[...], act[pair], preferred_element_type=F32)
+        return [both[0:CHAN], both[CHAN:2 * CHAN]]
 
     def update(tile, group, drifts):
         for i in range(GROUP):
@@ -147,28 +161,34 @@
             x = lat[tile, j] + hb[j] * drifts[i]
             lat[tile, j + 1] = x
             xb = x.astype(BF16)
+            slot = jnp.where(tile == TILES, STEPS + TILES, j + 1)
             for r in range(3):
-                rhs[j + 1, 16 * r:16 * r + 16, :] = xb
-
-    def phase_q(next_tile, next_group, first):
-        for i in range(HALF_GROUP):
-            product1(next_tile, next_group, 1, pre_b, i)
-        drifts = [] if first else [product2(act_b, i) for i in range(HALF_GROUP)]
-        for i in range(HALF_GROUP):
-            gelu(pre_a, act_a, i)
-        return drifts
-
-    def phase_p(next_tile, next_group):
-        for i in range(HALF_GROUP):
-            product1(next_tile, next_group, 0, pre_a, i)
-        drifts = [product2(act_a, i) for i in range(HALF_GROUP)]
-        for i in range(HALF_GROUP):
-            gelu(pre_b, act_b, i)
-        return drifts
-
-    for i in range(HALF_GROUP):
-        product1(0, 0, 0, pre_a, i)
-    phase_q(0, 0, True)
+                rhs[slot, 16 * r:16 * r + 16, :] = xb
+
+    pres, acts = [pre_a, pre_b], [act_a, act_b]
+
+    def split(index):
+        return lax.div(index, GROUPS), lax.rem(index, GROUPS)
+
+    def second_products(act):
+        return [d for i in range(GROUP // 2) for d in product2(act, i)]
+
+    def stage(index, parity):
+        next_tile, next_group = split(jnp.minimum(index + 1, TILES * GROUPS - 1))
+        drifts = []
+        for step in ORDER.split():
+            kind, i = step[0], int(step[1])
+            if kind == 'g':
+                gelu(pres[parity], acts[parity], i)
+            elif kind == 'p':
+                product1(next_tile, next_group, pres[1 - parity], i)
+            else:
+                drifts += product2(acts[1 - parity], i)
+        tile, group = split(jnp.maximum(index - 1, 0))
+        update(jnp.where(index == 0, TILES, tile), group, drifts)
+
+    for i in range(GROUP):
+        product1(0, 0, pre_a, i)
 
     def outgoing(tile, q, pm, slot):
         return pltpu.make_async_remote_copy(
@@ -178,34 +198,34 @@
             recv_sem=recv_sem.at[me, tile],
             device_id={"model": pm, "time": q}, device_id_type=MESH)
 
-    def trip(tile, group, c):
-        wrap = group == GROUPS - 1
-        next_tile = jnp.where(wrap, jnp.minimum(tile + 1, TILES - 1), tile)
-        next_group = jnp.where(wrap, 0, group + 1)
-        drifts = phase_p(next_tile, next_group)
-        drifts = drifts + phase_q(next_tile, next_group, False)
-        update(tile, group, drifts)
+    def send(tile, q):
+        outgoing(tile, q, 1 - m, 0).start()
+
+        @pl.when(q != t)
+        def _():
+            outgoing(tile, q, m, 1).start()
+
+        @pl.when(q == t)
+        def _():
+            for r in range(STEPS_DEV):
+                out_ref[r, me * TILES + tile] = lat[tile, q * STEPS_DEV + r]
+
+    def send_done(index):
+        tile, group = split(jnp.maximum(index - 1, 0))
 
         @pl.when(group >= GROUPS - 4)
         def _():
-            q = group - (GROUPS - 4)
-            outgoing(tile, q, 1 - m, 0).start()
-
-            @pl.when(q != t)
-            def _():
-                outgoing(tile, q, m, 1).start()
-
-            @pl.when(q == t)
-            def _():
-                for r in range(STEPS_DEV):
-                    out_ref[r, me * TILES + tile] = lat[tile, q * STEPS_DEV + r]
-
-        return c
-
-    def tile_loop(tile, c):
-        return lax.fori_loop(0, GROUPS, lambda group, cc: trip(tile, group, cc), c)
-
-    lax.fori_loop(0, TILES, tile_loop, 0)
+            send(tile, group - (GROUPS - 4))
+
+    def trip(i, c):
+        for parity in range(2):
+            stage(2 * i + parity, parity)
+            send_done(2 * i + parity)
+        return c
+
+    lax.fori_loop(0, TILES * GROUPS // 2, trip, 0)
+    update(TILES - 1, GROUPS - 1, second_products(act_b))
+    send(TILES - 1, 3)
 
     def finish(i, c):
         for q in range(4):
@@ -233,10 +253,11 @@
     def device_body(x_init, w_up, w_down, mod_scale, mod_shift, step_size):
         batch = x_init.shape[0]
         vmem = pl.BlockSpec(memory_space=pltpu.VMEM)
+        hbm = pl.BlockSpec(memory_space=pltpu.HBM)
         out = pl.pallas_call(
             kernel,
             out_shape=pltpu.VMEM((STEPS_DEV, batch, CHAN, TOKENS), F32),
-            in_specs=[vmem] * 6,
+            in_specs=[hbm] * 6,
             out_specs=vmem,
             scratch_shapes=[
                 pltpu.VMEM((2, 4, STEPS_DEV, HALF), BF16),
@@ -249,21 +270,24 @@
                 pltpu.VMEM((2, STEPS, 256), F32),
                 pltpu.VMEM((2, STEPS, 256), F32),
                 pltpu.VMEM((STEPS, HIDDEN, DEPTH), BF16),
-                pltpu.VMEM((STEPS + TILES, DEPTH, TOKENS), BF16),
-                pltpu.VMEM((HALF_GROUP, HIDDEN, TOKENS), F32),
-                pltpu.VMEM((HALF_GROUP, HIDDEN, TOKENS), F32),
-                pltpu.VMEM((HALF_GROUP, HIDDEN, TOKENS), BF16),
-                pltpu.VMEM((HALF_GROUP, HIDDEN, TOKENS), BF16),
-                pltpu.VMEM((TILES, STEPS, CHAN, TOKENS), F32),
+                pltpu.VMEM((STEPS + TILES + 1, DEPTH, TOKENS), BF16),
+                pltpu.VMEM((2 * CHAN, 2 * HIDDEN), BF16),
+                pltpu.VMEM((TILES, CHAN, TOKENS), F32),
+                pltpu.VMEM((GROUP, HIDDEN, TOKENS), F32),
+                pltpu.VMEM((GROUP, HIDDEN, TOKENS), F32),
+                pltpu.VMEM((GROUP // 2, 2 * HIDDEN, TOKENS), BF16),
+                pltpu.VMEM((GROUP // 2, 2 * HIDDEN, TOKENS), BF16),
+                pltpu.VMEM((TILES + 1, STEPS, CHAN, TOKENS), F32),
+                pltpu.SemaphoreType.DMA((6,)),
                 pltpu.SemaphoreType.DMA((19,)),
                 pltpu.SemaphoreType.DMA((19,)),
                 pltpu.SemaphoreType.DMA((TILES, 4, 2)),
                 pltpu.SemaphoreType.DMA((8, TILES)),
             ],
             compiler_params=pltpu.CompilerParams(
-                collective_id=0, has_side_effects=True, vmem_limit_bytes=24 * 1024 * 1024),
-        )(x_init.transpose(0, 2, 1), w_up, w_down.T, mod_scale, mod_shift,
-          step_size[None, :])
+                collective_id=0, has_side_effects=True, vmem_limit_bytes=32 * 1024 * 1024),
+        )(*[pltpu.with_memory_space_constraint(a, pltpu.HBM) for a in (
+            x_init.transpose(0, 2, 1), w_up, w_down.T, mod_scale, mod_shift, step_size[None, :])])
         return out.transpose(0, 1, 3, 2)
 
     return jax.shard_map(

time: 166 us -> 151 us (0.910)
  Pallas kernels: 158 us -> 147 us
  local copies, waits for them, and re-layouts: 8.04 us -> 3.4 us
    pallas_call x1, Pallas kernels: 158 us -> 147 us  [device_body(): pl.pallas_call(kernel, out_shape=pltpu.VMEM((STEPS_DEV, batch, CHAN, TOKE...]
    unnamed x13 -> x1, local copies, waits for them, and re-layouts: 8.04 us -> 3.4 us
where the time goes in v3:
time: 151 us
  Pallas kernels  147 us (97%)
  local copies, waits for them, and re-layouts  3.4 us (2%)
    pallas_call x1, Pallas kernels, device_body(): pl.pallas_call(kernel, out_shape=pltpu.VMEM((STEPS_DEV, batch, CHAN, TOKE...  147 us
    unnamed x1, local copies, waits for them, and re-layouts  3.4 us

profile of v3, /device:TPU:0, one launch (start us, length us, event | category | flops | bytes accessed | tf_op | source)
XLA Modules:
  0.0 150.8 jit_solution(1813029052968292446)
XLA Ops:
  0.0 147.4 %shard_map.64 = f32[8,64,16,256]{3,2,1,0:T(8,128)S(1)} custom-call(f32[64,16,256]{2,1,0:T(8,128)} %bitcast.5, bf16[16,192]{1,0:T(8,128)(2,1)} %w1_ref.1, bf16[16,192]{1,0:T(8,128)(2,1)} %bitcast.6, bf16[8,192]{1,0:T(8,128)(2,1)} %g_ref.1, bf16[8,192]{1,0:T(8,128)(2,1)} %b_ref.1, f32[1,8]{1,0:T(1,128)} %bitcast.7), custom_call_target="tpu_custom_call" | custom-call | tf_op jit(solution)/shard_map/pallas_call | solution.py:257
  147.4 3.4 %copy.8 = f32[8,64,256,16]{2,3,1,0:T(8,128)} copy(f32[8,64,256,16]{2,3,1,0:T(8,128)S(1)} %bitcast.4) | data formatting | bytes 16777216

commit v4 on v3

--- a/solution.py
+++ b/solution.py
@@ -20,9 +20,17 @@
 TOKENS = 256
 TILES = 8
 GROUP = 8
-GROUPS = 15
+ITEMS = 118
+GROUPS = TILES * ITEMS // GROUP
 DEPTH = 128
-ORDER = ('g0 p0 p1 g1 ' 'q0 q1 p2 g2 ' 'p3 q2 q3 g3 ' 'p4 p5 g4 p6 ' 'g5 p7 g6 g7')
+PARTS = 2
+PART = HIDDEN // PARTS
+ORDER = (
+    ('g', 0), ('p', 0), ('g', 1), ('p', 1), ('q', 0), ('g', 2), ('p', 2), ('g', 3), ('p', 3), ('q', 1),
+    ('g', 4), ('p', 4), ('g', 5), ('p', 5), ('q', 2), ('g', 6), ('p', 6), ('g', 7), ('p', 7), ('q', 3),
+    ('g', 8), ('p', 8), ('g', 9), ('p', 9), ('g', 10), ('p', 10), ('g', 11), ('p', 11), ('g', 12), ('p', 12),
+    ('g', 13), ('p', 13), ('g', 14), ('p', 14), ('p', 15), ('g', 15),
+)
 
 ROOT = math.sqrt(2.0 / math.pi)
 C1 = 2.0 * ROOT
@@ -30,10 +38,12 @@
 
 
 def item(group, k):
-    n = group * GROUP + k
-    sweep0 = n < 31
-    j = jnp.where(sweep0, n, jnp.where(n < 61, n - 30, jnp.where(n < 91, n - 60, n - 89)))
-    return sweep0, j
+    start = group * GROUP
+    tile, n = lax.div(start, ITEMS), lax.rem(start, ITEMS) + k
+    wrap = n >= ITEMS
+    tile, n = jnp.where(wrap, tile + 1, tile), jnp.where(wrap, n - ITEMS, n)
+    j = jnp.where(n < 31, n, jnp.where(n < 61, n - 30, jnp.where(n < 90, n - 59, n - 87)))
+    return tile, n < 31, j
 
 
 def kernel(x_ref, w1_ref, w2_ref, g_ref, b_ref, h_ref, out_ref,
@@ -135,16 +145,18 @@
             mat[j, HALF * mm:HALF * mm + HALF, :] = cols.T[0:HALF, :].astype(BF16)
         return c
 
-    lax.fori_loop(0, STEPS, prep, 0)
-
-    def product1(tile, group, pre, i):
-        sweep0, j = item(group, i)
+    lax.fori_loop(0, STEPS, prep, 0, unroll=4)
+
+    def product1(group, pre, h):
+        i, rows = h // PARTS, pl.ds(h % PARTS * PART, PART)
+        tile, sweep0, j = item(group, i)
         slot = jnp.where(sweep0, STEPS + tile, j)
-        pre[i] = jnp.dot(mat[j], rhs[slot], preferred_element_type=F32)
-
-    def gelu(pre, act, i):
+        pre[i, rows, :] = jnp.dot(mat[j, rows, :], rhs[slot], preferred_element_type=F32)
+
+    def gelu(pre, act, h):
+        i = h // PARTS
         u = i % 2
-        for r in range(0, HIDDEN, 16):
+        for r in range(h % PARTS * PART, h % PARTS * PART + PART, 16):
             part, k = r // HALF, r % HALF
             row = u * 256 + part * 128 + k if k < 128 else 512 + u * 128 + part * 64 + k - 128
             z = pre[i, r:r + 16, :]
@@ -155,47 +167,43 @@
         both = jnp.dot(w2p[...], act[pair], preferred_element_type=F32)
         return [both[0:CHAN], both[CHAN:2 * CHAN]]
 
-    def update(tile, group, drifts):
+    def update(group, spare, drifts):
         for i in range(GROUP):
-            _, j = item(group, i)
+            tile, _, j = item(group, i)
+            tile = jnp.where(spare, TILES, tile)
             x = lat[tile, j] + hb[j] * drifts[i]
             lat[tile, j + 1] = x
             xb = x.astype(BF16)
-            slot = jnp.where(tile == TILES, STEPS + TILES, j + 1)
+            slot = jnp.where(spare, STEPS + TILES, j + 1)
             for r in range(3):
                 rhs[slot, 16 * r:16 * r + 16, :] = xb
 
     pres, acts = [pre_a, pre_b], [act_a, act_b]
 
-    def split(index):
-        return lax.div(index, GROUPS), lax.rem(index, GROUPS)
-
     def second_products(act):
         return [d for i in range(GROUP // 2) for d in product2(act, i)]
 
     def stage(index, parity):
-        next_tile, next_group = split(jnp.minimum(index + 1, TILES * GROUPS - 1))
+        following = jnp.minimum(index + 1, GROUPS - 1)
         drifts = []
-        for step in ORDER.split():
-            kind, i = step[0], int(step[1])
+        for kind, i in ORDER:
             if kind == 'g':
                 gelu(pres[parity], acts[parity], i)
             elif kind == 'p':
-                product1(next_tile, next_group, pres[1 - parity], i)
+                product1(following, pres[1 - parity], i)
             else:
                 drifts += product2(acts[1 - parity], i)
-        tile, group = split(jnp.maximum(index - 1, 0))
-        update(jnp.where(index == 0, TILES, tile), group, drifts)
-
-    for i in range(GROUP):
-        product1(0, 0, pre_a, i)
+        update(jnp.maximum(index - 1, 0), index == 0, drifts)
+
+    for h in range(PARTS * GROUP):
+        product1(0, pre_a, h)
 
     def outgoing(tile, q, pm, slot):
         return pltpu.make_async_remote_copy(
             src_ref=lat.at[tile, pl.ds(q * STEPS_DEV, STEPS_DEV)],
             dst_ref=out_ref.at[:, me * TILES + tile],
-            send_sem=send_sem.at[tile, q, slot],
-            recv_sem=recv_sem.at[me, tile],
+            send_sem=send_sem.at[q, slot],
+            recv_sem=recv_sem.at[me],
             device_id={"model": pm, "time": q}, device_id_type=MESH)
 
     def send(tile, q):
@@ -210,43 +218,43 @@
             for r in range(STEPS_DEV):
                 out_ref[r, me * TILES + tile] = lat[tile, q * STEPS_DEV + r]
 
-    def send_done(index):
-        tile, group = split(jnp.maximum(index - 1, 0))
-
-        @pl.when(group >= GROUPS - 4)
-        def _():
-            send(tile, group - (GROUPS - 4))
+    def send_done(group):
+        past = jnp.maximum(group * GROUP + GROUP - 1 - 93, 0)
+        tile, rest = lax.div(past, ITEMS), lax.rem(past, ITEMS)
+
+        @pl.when((group * GROUP + GROUP - 1 >= 93) & (rest < 32))
+        def _():
+            send(tile, lax.div(rest, 8))
 
     def trip(i, c):
         for parity in range(2):
             stage(2 * i + parity, parity)
-            send_done(2 * i + parity)
+            send_done(2 * i + parity - 1)
         return c
 
-    lax.fori_loop(0, TILES * GROUPS // 2, trip, 0)
-    update(TILES - 1, GROUPS - 1, second_products(act_b))
+    lax.fori_loop(0, GROUPS // 2, trip, 0)
+    update(GROUPS - 1, False, second_products(act_b))
     send(TILES - 1, 3)
 
-    def finish(i, c):
-        for q in range(4):
-            outgoing(i, q, 1 - m, 0).wait_send()
-
-            @pl.when(q != t)
-            def _():
-                outgoing(i, q, m, 1).wait_send()
-
-        for src in range(8):
-            @pl.when(src != me)
-            def _():
-                pltpu.make_async_remote_copy(
-                    src_ref=lat.at[0, pl.ds(0, STEPS_DEV)],
-                    dst_ref=out_ref.at[:, src * TILES + i],
-                    send_sem=send_sem.at[0, 0, 0],
-                    recv_sem=recv_sem.at[src, i],
-                    device_id={"model": m, "time": t}, device_id_type=MESH).wait_recv()
-        return c
-
-    lax.fori_loop(0, TILES, finish, 0)
+    def waiter(q, slot, src):
+        return pltpu.make_async_remote_copy(
+            src_ref=lat.at[pl.ds(0, TILES), pl.ds(q * STEPS_DEV, STEPS_DEV)],
+            dst_ref=out_ref.at[:, pl.ds(src * TILES, TILES)],
+            send_sem=send_sem.at[q, slot],
+            recv_sem=recv_sem.at[src],
+            device_id={"model": 1 - m, "time": t}, device_id_type=MESH)
+
+    for q in range(4):
+        waiter(q, 0, 0).wait_send()
+
+        @pl.when(q != t)
+        def _():
+            waiter(q, 1, 0).wait_send()
+
+    for src in range(8):
+        @pl.when(src != me)
+        def _():
+            waiter(0, 0, src).wait_recv()
 
 
 def solution(mesh):
@@ -281,8 +289,8 @@
                 pltpu.SemaphoreType.DMA((6,)),
                 pltpu.SemaphoreType.DMA((19,)),
                 pltpu.SemaphoreType.DMA((19,)),
-                pltpu.SemaphoreType.DMA((TILES, 4, 2)),
-                pltpu.SemaphoreType.DMA((8, TILES)),
+                pltpu.SemaphoreType.DMA((4, 2)),
+                pltpu.SemaphoreType.DMA((8,)),
             ],
             compiler_params=pltpu.CompilerParams(
                 collective_id=0, has_side_effects=True, vmem_limit_bytes=32 * 1024 * 1024),

time: 151 us -> 134 us (0.89)
  Pallas kernels: 147 us -> 130 us
    pallas_call x1, Pallas kernels: 147 us -> 130 us  [device_body(): pl.pallas_call(kernel, out_shape=pltpu.VMEM((STEPS_DEV, batch, CHAN, TOKE...]
where the time goes in v4:
time: 134 us
  Pallas kernels  130 us (97%)
  local copies, waits for them, and re-layouts  3.4 us (3%)
    pallas_call x1, Pallas kernels, device_body(): pl.pallas_call(kernel, out_shape=pltpu.VMEM((STEPS_DEV, batch, CHAN, TOKE...  130 us
    unnamed x1, local copies, waits for them, and re-layouts  3.4 us

profile of v4, /device:TPU:0, one launch (start us, length us, event | category | flops | bytes accessed | tf_op | source)
XLA Modules:
  0.0 133.8 jit_solution(10809580254420428111)
XLA Ops:
  0.0 130.4 %shard_map.64 = f32[8,64,16,256]{3,2,1,0:T(8,128)S(1)} custom-call(f32[64,16,256]{2,1,0:T(8,128)} %bitcast.5, bf16[16,192]{1,0:T(8,128)(2,1)} %w1_ref.1, bf16[16,192]{1,0:T(8,128)(2,1)} %bitcast.6, bf16[8,192]{1,0:T(8,128)(2,1)} %g_ref.1, bf16[8,192]{1,0:T(8,128)(2,1)} %b_ref.1, f32[1,8]{1,0:T(1,128)} %bitcast.7), custom_call_target="tpu_custom_call" | custom-call | tf_op jit(solution)/shard_map/pallas_call | solution.py:265
  130.4 3.4 %copy.8 = f32[8,64,256,16]{2,3,1,0:T(8,128)} copy(f32[8,64,256,16]{2,3,1,0:T(8,128)S(1)} %bitcast.4) | data formatting | bytes 16777216

commit v5 on v4

--- a/solution.py
+++ b/solution.py
@@ -26,10 +26,10 @@
 PARTS = 2
 PART = HIDDEN // PARTS
 ORDER = (
-    ('g', 0), ('p', 0), ('g', 1), ('p', 1), ('q', 0), ('g', 2), ('p', 2), ('g', 3), ('p', 3), ('q', 1),
-    ('g', 4), ('p', 4), ('g', 5), ('p', 5), ('q', 2), ('g', 6), ('p', 6), ('g', 7), ('p', 7), ('q', 3),
-    ('g', 8), ('p', 8), ('g', 9), ('p', 9), ('g', 10), ('p', 10), ('g', 11), ('p', 11), ('g', 12), ('p', 12),
-    ('g', 13), ('p', 13), ('g', 14), ('p', 14), ('p', 15), ('g', 15),
+    ('g', 0), ('p', 0), ('q', 0), ('g', 1), ('p', 1), ('p', 2), ('g', 2), ('p', 3), ('g', 3), ('q', 1),
+    ('p', 4), ('g', 4), ('p', 5), ('g', 5), ('p', 6), ('q', 2), ('g', 6), ('p', 7), ('g', 7), ('p', 8),
+    ('g', 8), ('q', 3), ('p', 9), ('g', 9), ('p', 10), ('g', 10), ('p', 11), ('g', 11), ('p', 12), ('g', 12),
+    ('p', 13), ('g', 13), ('p', 14), ('g', 14), ('p', 15), ('g', 15),
 )
 
 ROOT = math.sqrt(2.0 / math.pi)

time: 134 us -> 129 us (0.963)
  Pallas kernels: 130 us -> 126 us
    pallas_call x1, Pallas kernels: 130 us -> 126 us  [device_body(): pl.pallas_call(kernel, out_shape=pltpu.VMEM((STEPS_DEV, batch, CHAN, TOKE...]
where the time goes in v5:
time: 129 us
  Pallas kernels  126 us (98%)
  local copies, waits for them, and re-layouts  3.4 us (3%)
    pallas_call x1, Pallas kernels, device_body(): pl.pallas_call(kernel, out_shape=pltpu.VMEM((STEPS_DEV, batch, CHAN, TOKE...  126 us
    unnamed x1, local copies, waits for them, and re-layouts  3.4 us

profile of v5, /device:TPU:0, one launch (start us, length us, event | category | flops | bytes accessed | tf_op | source)
XLA Modules:
  0.0 129.2 jit_solution(7810198658474882234)
XLA Ops:
  0.0 125.8 %shard_map.64 = f32[8,64,16,256]{3,2,1,0:T(8,128)S(1)} custom-call(f32[64,16,256]{2,1,0:T(8,128)} %bitcast.5, bf16[16,192]{1,0:T(8,128)(2,1)} %w1_ref.1, bf16[16,192]{1,0:T(8,128)(2,1)} %bitcast.6, bf16[8,192]{1,0:T(8,128)(2,1)} %g_ref.1, bf16[8,192]{1,0:T(8,128)(2,1)} %b_ref.1, f32[1,8]{1,0:T(1,128)} %bitcast.7), custom_call_target="tpu_custom_call" | custom-call | tf_op jit(solution)/shard_map/pallas_call | solution.py:265
  125.8 3.4 %copy.8 = f32[8,64,256,16]{2,3,1,0:T(8,128)} copy(f32[8,64,256,16]{2,3,1,0:T(8,128)S(1)} %bitcast.4) | data formatting | bytes 16777216

commit v6 on v5

--- a/solution.py
+++ b/solution.py
@@ -26,9 +26,9 @@
 PARTS = 2
 PART = HIDDEN // PARTS
 ORDER = (
-    ('g', 0), ('p', 0), ('q', 0), ('g', 1), ('p', 1), ('p', 2), ('g', 2), ('p', 3), ('g', 3), ('q', 1),
+    ('g', 0), ('q', 0), ('g', 1), ('p', 0), ('p', 1), ('p', 2), ('g', 2), ('p', 3), ('g', 3), ('q', 1),
     ('p', 4), ('g', 4), ('p', 5), ('g', 5), ('p', 6), ('q', 2), ('g', 6), ('p', 7), ('g', 7), ('p', 8),
-    ('g', 8), ('q', 3), ('p', 9), ('g', 9), ('p', 10), ('g', 10), ('p', 11), ('g', 11), ('p', 12), ('g', 12),
+    ('g', 8), ('q', 3), ('p', 9), ('g', 9), ('p', 10), ('g', 10), ('g', 11), ('p', 11), ('p', 12), ('g', 12),
     ('p', 13), ('g', 13), ('p', 14), ('g', 14), ('p', 15), ('g', 15),
 )
 

time: 129 us -> 128 us (level)
  Pallas kernels: 126 us -> 124 us
    pallas_call x1, Pallas kernels: 126 us -> 124 us  [device_body(): pl.pallas_call(kernel, out_shape=pltpu.VMEM((STEPS_DEV, batch, CHAN, TOKE...]
where the time goes in v6:
time: 128 us
  Pallas kernels  124 us (97%)
  local copies, waits for them, and re-layouts  3.4 us (3%)
    pallas_call x1, Pallas kernels, device_body(): pl.pallas_call(kernel, out_shape=pltpu.VMEM((STEPS_DEV, batch, CHAN, TOKE...  124 us
    unnamed x1, local copies, waits for them, and re-layouts  3.4 us

profile of v6, /device:TPU:0, one launch (start us, length us, event | category | flops | bytes accessed | tf_op | source)
XLA Modules:
  0.0 127.7 jit_solution(15971480621145975571)
XLA Ops:
  0.0 124.3 %shard_map.64 = f32[8,64,16,256]{3,2,1,0:T(8,128)S(1)} custom-call(f32[64,16,256]{2,1,0:T(8,128)} %bitcast.5, bf16[16,192]{1,0:T(8,128)(2,1)} %w1_ref.1, bf16[16,192]{1,0:T(8,128)(2,1)} %bitcast.6, bf16[8,192]{1,0:T(8,128)(2,1)} %g_ref.1, bf16[8,192]{1,0:T(8,128)(2,1)} %b_ref.1, f32[1,8]{1,0:T(1,128)} %bitcast.7), custom_call_target="tpu_custom_call" | custom-call | tf_op jit(solution)/shard_map/pallas_call | solution.py:265
  124.3 3.4 %copy.8 = f32[8,64,256,16]{2,3,1,0:T(8,128)} copy(f32[8,64,256,16]{2,3,1,0:T(8,128)S(1)} %bitcast.4) | data formatting | bytes 16777216

commit v7 on v6

--- a/solution.py
+++ b/solution.py
@@ -145,7 +145,7 @@
             mat[j, HALF * mm:HALF * mm + HALF, :] = cols.T[0:HALF, :].astype(BF16)
         return c
 
-    lax.fori_loop(0, STEPS, prep, 0, unroll=4)
+    lax.fori_loop(0, STEPS, prep, 0, unroll=8)
 
     def product1(group, pre, h):
         i, rows = h // PARTS, pl.ds(h % PARTS * PART, PART)

time: 128 us -> 128 us (level)
  no operation moved by 1% of the time
where the time goes in v7:
time: 128 us; the launch traced here: 127 us
  Pallas kernels  124 us (97%)
  local copies, waits for them, and re-layouts  3.4 us (3%)
    pallas_call x1, Pallas kernels, device_body(): pl.pallas_call(kernel, out_shape=pltpu.VMEM((STEPS_DEV, batch, CHAN, TOKE...  124 us
    unnamed x1, local copies, waits for them, and re-layouts  3.4 us

profile of v7, /device:TPU:0, one launch (start us, length us, event | category | flops | bytes accessed | tf_op | source)
XLA Modules:
  0.0 127.4 jit_solution(8022469222192339922)
XLA Ops:
  0.0 124.0 %shard_map.64 = f32[8,64,16,256]{3,2,1,0:T(8,128)S(1)} custom-call(f32[64,16,256]{2,1,0:T(8,128)} %bitcast.5, bf16[16,192]{1,0:T(8,128)(2,1)} %w1_ref.1, bf16[16,192]{1,0:T(8,128)(2,1)} %bitcast.6, bf16[8,192]{1,0:T(8,128)(2,1)} %g_ref.1, bf16[8,192]{1,0:T(8,128)(2,1)} %b_ref.1, f32[1,8]{1,0:T(1,128)} %bitcast.7), custom_call_target="tpu_custom_call" | custom-call | tf_op jit(solution)/shard_map/pallas_call | solution.py:265
  124.0 3.4 %copy.8 = f32[8,64,256,16]{2,3,1,0:T(8,128)} copy(f32[8,64,256,16]{2,3,1,0:T(8,128)S(1)} %bitcast.4) | data formatting | bytes 16777216
